TPU v7x, 32 devices: a whole 2x2x4 slice. The times are simulated.
32 devices in a mesh: gx: 4 (over y, x), gy: 4 (over z), gz: 2 (over core).
Axes of the slice: x: 2, y: 2, z: 4, core: 2. Of those that a mesh axis runs over, the one named last changes fastest.
Arguments:
- fields: bfloat16 [4096, 2048], P(('gx', 'gy', 'gz')), may hold values from -6 to 6
- coordinates: float32 [3, 524288], P(None, ('gx', 'gy', 'gz')), may hold values from -1 to 1
- element_rank: int32 [524288, 1], P(('gx', 'gy', 'gz')), may hold values from 0 to 31; in each aligned block of 16384 rows (0 to 16383, 16384 to 32767, ...) at most 640 rows name the same one
- element_slot: int32 [524288], P(('gx', 'gy', 'gz')), may hold values from 0 to 127
Outputs:
- samples: float32 [4, 524288], P(None, ('gx', 'gy', 'gz'))
Inputs may be any that keep to these rules, and one draw needn't show every extreme that they name: `element_rank`: among the probes of one device no rank is named by more than 640 probes, and in some devices' blocks one rank is named by exactly 640.
All inputs are finite; a program needn't handle non-finite values.
Results may differ from a plain program's by a relative error of at most 0.0024.
Values sent between devices are 32-bit elements; how exact they have to be, the bound alone decides.
No kernel may reach another device: no remote copies, remote signals or barrier semaphores. Data moves between devices by JAX's collectives and lax.ppermute only.
A program may use at most 64 MiB of HBM per device.

v0:
```python
import math
import jax
import jax.numpy as jnp
import numpy as np
from jax import lax
from jax.sharding import PartitionSpec as P

gll_points = np.array(
    [
        -1.0,
        -0.8717401485096066,
        -0.5917001814331423,
        -0.2092992179024789,
        0.2092992179024789,
        0.5917001814331423,
        0.8717401485096066,
        1.0,
    ]
)
gll_scale = np.array(
    [1.0 / np.prod([gll_points[a] - gll_points[b] for b in range(8) if b != a]) for a in range(8)]
)


def lagrange(coord):
    offsets = coord[None, :] - jnp.asarray(gll_points, coord.dtype)[:, None]
    weights = []
    for node_a in range(8):
        factor = jnp.ones_like(coord) * gll_scale[node_a]
        for node_b in range(8):
            if node_b != node_a:
                factor = factor * offsets[node_b]
        weights.append(factor)
    return jnp.stack(weights, axis=0)


def interpolate(payload, fields):
    total_rows = payload.shape[1]
    local_count = fields.shape[0]
    block_rows = math.gcd(total_rows, 2048)
    block_count = total_rows // block_rows
    element_ids = jnp.arange(local_count, dtype=jnp.int32)

    def one_block(block):
        weight_r = lagrange(block[0])
        weight_s = lagrange(block[1])
        weight_t = lagrange(block[2]).astype(jnp.bfloat16)
        slots_block = block[3].astype(jnp.int32)
        picker = (slots_block[:, None] == element_ids[None, :]).astype(jnp.bfloat16)
        gathered = jnp.dot(picker, fields, preferred_element_type=jnp.float32).astype(jnp.bfloat16)
        gathered = gathered.reshape(block_rows, 256, 8)
        along_t = jnp.einsum("nak,kn->na", gathered, weight_t, preferred_element_type=jnp.float32)
        along_t = along_t.reshape(block_rows, 4, 8, 8)
        along_s = jnp.einsum("nfij,jn->nfi", along_t, weight_s, precision=lax.Precision.HIGHEST)
        return jnp.einsum("nfi,in->fn", along_s, weight_r, precision=lax.Precision.HIGHEST)

    blocks = payload.reshape(4, block_count, block_rows).transpose(1, 0, 2)
    result = lax.map(one_block, blocks)
    return result.transpose(1, 0, 2).reshape(4, total_rows)


def local(fields, coordinates, element_rank, element_slot):
    devices = lax.axis_size(("gx", "gy", "gz"))
    probes = element_slot.shape[0]
    capacity = 5 * probes // (4 * devices)
    target = element_rank[:, 0]
    group_rows = math.gcd(probes, 512)
    group_count = probes // group_rows
    onehot = (target[:, None] == jnp.arange(devices, dtype=jnp.int32)[None, :]).astype(jnp.bfloat16)
    onehot = onehot.reshape(group_count, group_rows, devices)
    lower = jnp.arange(group_rows)
    triangle = (lower[:, None] >= lower[None, :]).astype(jnp.bfloat16)
    within = jnp.einsum("ij,bjd->bid", triangle, onehot, preferred_element_type=jnp.float32)
    totals = within[:, -1, :]
    offsets = jnp.cumsum(totals, axis=0) - totals
    counted = (within + offsets[:, None, :]) * onehot.astype(jnp.float32)
    position = (jnp.sum(counted, axis=2).reshape(probes) - 1.0).astype(jnp.int32)
    flat = target * capacity + position
    payload = jnp.concatenate([coordinates, element_slot.astype(jnp.float32)[None, :]], axis=0)
    send = jnp.zeros((4, devices * capacity), jnp.float32).at[:, flat].set(payload)
    arrived = lax.all_to_all(
        send.reshape(4, devices, capacity),
        ("gx", "gy", "gz"),
        split_axis=1,
        concat_axis=1,
        tiled=True,
    )
    width = arrived.shape[2]
    values = interpolate(arrived.reshape(4, -1), fields)
    values = values.reshape(4, devices, width)
    returned = lax.all_to_all(values, ("gx", "gy", "gz"), split_axis=1, concat_axis=1, tiled=True)
    return returned.reshape(4, devices * capacity)[:, flat]


def solution(mesh):
    placed = (
        P(("gx", "gy", "gz"), None),
        P(None, ("gx", "gy", "gz")),
        P(("gx", "gy", "gz"), None),
        P(("gx", "gy", "gz")),
    )
    return jax.shard_map(
        local, mesh=mesh, in_specs=placed, out_specs=P(None, ("gx", "gy", "gz")), check_vma=False
    )
```

profile of v0, /device:TPU:0, one launch (start us, length us, event | category | flops | bytes accessed | tf_op | source)
XLA Modules:
  0.0 265.9 jit_solution(6529468678508932925)
XLA Ops:
  0.5 1.6 reduce.11
  2.2 0.8 fusion.8
  5.1 5.1 %copy.32 = f32[16384,4]{1,0:T(8,128)} copy(f32[16384,4]{0,1:T(4,128)S(1)} %maximum_bitcast_fusion) | data formatting | bytes 524288 | tf_op jit(solution)/shard_map/concatenate | solution.py:79
  10.2 45.3 %scatter_custom_fusion = f32[4,20480]{0,1:T(8,128)} fusion(s32[16384]{0:T(1024)S(1)} %bitcast.89, f32[16384,4]{1,0:T(8,128)} %copy.32, f32[]{:T(128)} %constant.13.clone.1), kind=kCustom, calls=%fused_computation.42 | custom fusion | bytes 328192 | tf_op jit(solution)/shard_map/scatter | solution.py:80
  55.6 6.7 %copy.33 = f32[4,32,640]{2,0,1:T(4,128)} copy(f32[4,32,640]{0,2,1:T(8,128)} %bitcast.80) | data formatting | bytes 655360 | tf_op jit(solution)/shard_map/reshape | solution.py:82
  62.2 7.5 %all-to-all-start = ((f32[4,32,640]{2,0,1:T(4,128)}), f32[4,32,640]{2,0,1:T(4,128)S(1)}, u32[]{:S(2)}, u32[]{:S(2)}) async-start(f32[4,32,640]{2,0,1:T(4,128)} %copy.33), calls=%async_computation | async-start | bytes 655360 | tf_op jit(solution)/shard_map/all_to_all | solution.py:81
  69.8 11.8 %all-to-all-done = f32[4,32,640]{2,0,1:T(4,128)S(1)} async-done(((f32[4,32,640]{2,0,1:T(4,128)}), f32[4,32,640]{2,0,1:T(4,128)S(1)}, u32[]{:S(2)}, u32[]{:S(2)}) %all-to-all-start) | async-done | bytes 327712 | tf_op jit(solution)/shard_map/all_to_all | solution.py:81
  81.7 99.4 %while.13 = (s32[]{:T(128)}, f32[10,4,2048]{2,1,0:T(4,128)}, f32[10,4,2048]{2,0,1:T(8,128)S(1)}, bf16[128,2048]{1,0:T(8,128)(2,1)}, s32[]{:T(128)}, /*index=5*/f32[8]{0:T(128)S(1)}, s32[]{:T(128)}, s32[]{}, s32[]{}, s32[]{}) while((s32[]{:T(128)}, f32[10,4,2048]{2,1,0:T(4,128)}, ...), condition=%wide.region_4.5_spmd.clone.clone.clone, body=%wide.region_3.4_spmd.sunk.clone.clone.clone.sunk | while | flops 1091790848 | bytes 7209657 | solution.py:58
  82.3 7.2 %multiply_reduce_fusion.7 = f32[2048,256]{0,1:T(8,128)S(1)} fusion(f32[2048,8]{0,1:T(8,128)S(1)} %bitcast_convert_fusion.2, bf16[128,2048]{1,0:T(8,128)(2,1)} %get-tuple-element.256, s32[2048]{0:T(1024)S(1)} %bitcast.93), kind=kOutput, calls=%fused_computation.3.clone.1 | convolution fusion | flops 1090256896 | bytes 2695168 | tf_op jit(solution)/shard_map/while/body/eval_jaxpr/dot_general | solution.py:50
  92.2 7.2 %multiply_reduce_fusion.7 = f32[2048,256]{0,1:T(8,128)S(1)} fusion(f32[2048,8]{0,1:T(8,128)S(1)} %bitcast_convert_fusion.2, bf16[128,2048]{1,0:T(8,128)(2,1)} %get-tuple-element.256, s32[2048]{0:T(1024)S(1)} %bitcast.93), kind=kOutput, calls=%fused_computation.3.clone.1 | convolution fusion | flops 1090256896 | bytes 2695168 | tf_op jit(solution)/shard_map/while/body/eval_jaxpr/dot_general | solution.py:50
  102.2 7.2 %multiply_reduce_fusion.7 = f32[2048,256]{0,1:T(8,128)S(1)} fusion(f32[2048,8]{0,1:T(8,128)S(1)} %bitcast_convert_fusion.2, bf16[128,2048]{1,0:T(8,128)(2,1)} %get-tuple-element.256, s32[2048]{0:T(1024)S(1)} %bitcast.93), kind=kOutput, calls=%fused_computation.3.clone.1 | convolution fusion | flops 1090256896 | bytes 2695168 | tf_op jit(solution)/shard_map/while/body/eval_jaxpr/dot_general | solution.py:50
  109.7 0.7 multiply_reduce_fusion.8
  112.1 7.2 %multiply_reduce_fusion.7 = f32[2048,256]{0,1:T(8,128)S(1)} fusion(f32[2048,8]{0,1:T(8,128)S(1)} %bitcast_convert_fusion.2, bf16[128,2048]{1,0:T(8,128)(2,1)} %get-tuple-element.256, s32[2048]{0:T(1024)S(1)} %bitcast.93), kind=kOutput, calls=%fused_computation.3.clone.1 | convolution fusion | flops 1090256896 | bytes 2695168 | tf_op jit(solution)/shard_map/while/body/eval_jaxpr/dot_general | solution.py:50
  122.1 7.2 %multiply_reduce_fusion.7 = f32[2048,256]{0,1:T(8,128)S(1)} fusion(f32[2048,8]{0,1:T(8,128)S(1)} %bitcast_convert_fusion.2, bf16[128,2048]{1,0:T(8,128)(2,1)} %get-tuple-element.256, s32[2048]{0:T(1024)S(1)} %bitcast.93), kind=kOutput, calls=%fused_computation.3.clone.1 | convolution fusion | flops 1090256896 | bytes 2695168 | tf_op jit(solution)/shard_map/while/body/eval_jaxpr/dot_general | solution.py:50
  132.0 7.2 %multiply_reduce_fusion.7 = f32[2048,256]{0,1:T(8,128)S(1)} fusion(f32[2048,8]{0,1:T(8,128)S(1)} %bitcast_convert_fusion.2, bf16[128,2048]{1,0:T(8,128)(2,1)} %get-tuple-element.256, s32[2048]{0:T(1024)S(1)} %bitcast.93), kind=kOutput, calls=%fused_computation.3.clone.1 | convolution fusion | flops 1090256896 | bytes 2695168 | tf_op jit(solution)/shard_map/while/body/eval_jaxpr/dot_general | solution.py:50
  141.9 7.2 %multiply_reduce_fusion.7 = f32[2048,256]{0,1:T(8,128)S(1)} fusion(f32[2048,8]{0,1:T(8,128)S(1)} %bitcast_convert_fusion.2, bf16[128,2048]{1,0:T(8,128)(2,1)} %get-tuple-element.256, s32[2048]{0:T(1024)S(1)} %bitcast.93), kind=kOutput, calls=%fused_computation.3.clone.1 | convolution fusion | flops 1090256896 | bytes 2695168 | tf_op jit(solution)/shard_map/while/body/eval_jaxpr/dot_general | solution.py:50
  151.9 7.2 %multiply_reduce_fusion.7 = f32[2048,256]{0,1:T(8,128)S(1)} fusion(f32[2048,8]{0,1:T(8,128)S(1)} %bitcast_convert_fusion.2, bf16[128,2048]{1,0:T(8,128)(2,1)} %get-tuple-element.256, s32[2048]{0:T(1024)S(1)} %bitcast.93), kind=kOutput, calls=%fused_computation.3.clone.1 | convolution fusion | flops 1090256896 | bytes 2695168 | tf_op jit(solution)/shard_map/while/body/eval_jaxpr/dot_general | solution.py:50
  161.8 7.2 %multiply_reduce_fusion.7 = f32[2048,256]{0,1:T(8,128)S(1)} fusion(f32[2048,8]{0,1:T(8,128)S(1)} %bitcast_convert_fusion.2, bf16[128,2048]{1,0:T(8,128)(2,1)} %get-tuple-element.256, s32[2048]{0:T(1024)S(1)} %bitcast.93), kind=kOutput, calls=%fused_computation.3.clone.1 | convolution fusion | flops 1090256896 | bytes 2695168 | tf_op jit(solution)/shard_map/while/body/eval_jaxpr/dot_general | solution.py:50
  171.7 7.2 %multiply_reduce_fusion.7 = f32[2048,256]{0,1:T(8,128)S(1)} fusion(f32[2048,8]{0,1:T(8,128)S(1)} %bitcast_convert_fusion.2, bf16[128,2048]{1,0:T(8,128)(2,1)} %get-tuple-element.256, s32[2048]{0:T(1024)S(1)} %bitcast.93), kind=kOutput, calls=%fused_computation.3.clone.1 | convolution fusion | flops 1090256896 | bytes 2695168 | tf_op jit(solution)/shard_map/while/body/eval_jaxpr/dot_general | solution.py:50
  181.1 2.6 all-to-all-start.1
  183.8 12.0 %all-to-all-done.1 = f32[4,32,640]{2,0,1:T(4,128)S(1)} async-done(((f32[4,32,640]{2,0,1:T(4,128)}), f32[4,32,640]{2,0,1:T(4,128)S(1)}, u32[]{:S(2)}, u32[]{:S(2)}) %all-to-all-start.1) | async-done | bytes 327712 | tf_op jit(solution)/shard_map/all_to_all | solution.py:91
  195.8 5.5 %copy.38 = f32[4,32,640]{0,2,1:T(8,128)} copy(f32[4,32,640]{2,0,1:T(4,128)S(1)} %all-to-all-done.1) | data formatting | bytes 655360 | tf_op jit(solution)/shard_map/all_to_all | solution.py:91
  201.2 58.7 %gather_fusion = f32[16384,4]{1,0:T(8,128)} fusion(f32[4,20480]{0,1:T(8,128)} %bitcast.81, s32[16384]{0:T(1024)S(1)} %broadcast_clamp_fusion), kind=kCustom, calls=%fused_computation | custom fusion | bytes 589824 | tf_op jit(solution)/shard_map/gather | solution.py:92
  259.9 5.9 %copy.39 = f32[4,16384]{1,0:T(4,128)} copy(f32[4,16384]{0,1:T(8,128)} %bitcast.82) | data formatting | bytes 524288 | tf_op jit(solution)/shard_map/gather | solution.py:92
  (234 shorter events, 28.7 us)
Async XLA Ops:
  0.0 4.8 %copy-start = (s32[16384,1]{0,1:T(1,128)S(1)}, s32[16384,1]{0,1:T(1,128)}, u32[]{:S(2)}) copy-start(s32[16384,1]{0,1:T(1,128)} %param.11) | copy-start | bytes 196612
  0.0 5.0 %copy-start.2 = (s32[16384]{0:T(1024)S(1)}, s32[16384]{0:T(1024)}, u32[]{:S(2)}) copy-start(s32[16384]{0:T(1024)} %param.12) | copy-start | bytes 196612
  0.0 5.0 %copy-start.1 = (f32[3,16384]{1,0:T(4,128)S(1)}, f32[3,16384]{1,0:T(4,128)}, u32[]{:S(2)}) copy-start(f32[3,16384]{1,0:T(4,128)} %param.10) | copy-start | bytes 589828
  55.6 26.2 %copy-start.3 = (f32[8]{0:T(128)S(1)}, f32[8]{0:T(128)}, u32[]{:S(2)}) copy-start(f32[8]{0:T(128)} %constant.81) | copy-start | bytes 100
  62.2 19.4 %all-to-all-start = ((f32[4,32,640]{2,0,1:T(4,128)}), f32[4,32,640]{2,0,1:T(4,128)S(1)}, u32[]{:S(2)}, u32[]{:S(2)}) async-start(f32[4,32,640]{2,0,1:T(4,128)} %copy.33), calls=%async_computation | async-start | bytes 655360 | tf_op jit(solution)/shard_map/all_to_all | solution.py:81
  181.1 14.6 %all-to-all-start.1 = ((f32[4,32,640]{2,0,1:T(4,128)}), f32[4,32,640]{2,0,1:T(4,128)S(1)}, u32[]{:S(2)}, u32[]{:S(2)}) async-start(f32[4,32,640]{2,0,1:T(4,128)} %bitcast.14), calls=%async_computation.1 | async-start | bytes 655360 | tf_op jit(solution)/shard_map/all_to_all | solution.py:91
where the time goes:
time: 267 us; the launch traced here: 266 us
  local copies, waits for them, and re-layouts  138 us (52%)
  matrix products  72.3 us (27%)
  waiting for transfers between devices  23.8 us (9%)
  other arithmetic  20.2 us (8%)
  starting transfers between devices  10.1 us (4%)
    dot_general x10, matrix products, one_block(): jnp.dot(picker, fields, preferred_element_type=jnp.float32)  71.5 us
    gather x2, local copies, waits for them, and re-layouts, local(): return returned.reshape(4, devices * capacity)[:, flat]  64.6 us
    scatter x1, local copies, waits for them, and re-layouts, local(): jnp.zeros((4, devices * capacity), jnp.float32).at[:, flat].set(payload)  45.3 us
    all_to_all x1, waiting for transfers between devices, local(): lax.all_to_all(values, ('gx', 'gy', 'gz'), split_axis=1, concat_axis=1, t...  12 us
    all_to_all x1, waiting for transfers between devices, local(): lax.all_to_all(send.reshape(4, devices, capacity), ('gx', 'gy', 'gz'), sp...  11.8 us
    all_to_all x1, starting transfers between devices, local(): lax.all_to_all(send.reshape(4, devices, capacity), ('gx', 'gy', 'gz'), sp...  7.51 us
    dot_general x10, other arithmetic, one_block(): jnp.einsum('nfij,jn->nfi', along_t, weight_s, precision=lax.Precision.HIG...  6.96 us
    reshape x1, local copies, waits for them, and re-layouts, local(): send.reshape(4, devices, capacity)  6.68 us
  transfers between devices with their start and end apart: 2, of which 2 were waited for; matrix products, arithmetic and copies ran while one was open for 0% of the time, Pallas kernels for 0%

commit v1 on v0

--- a/solution.py
+++ b/solution.py
@@ -20,6 +20,12 @@
 gll_scale = np.array(
     [1.0 / np.prod([gll_points[a] - gll_points[b] for b in range(8) if b != a]) for a in range(8)]
 )
+
+
+def trade_parts(x, name, split, join):
+    pieces = jnp.split(x, lax.axis_size(name), axis=split)
+    received = lax.all_to_all(jnp.stack(pieces), name, 0, 0)
+    return jnp.concatenate(received, axis=join)
 
 
 def lagrange(coord):
@@ -78,13 +84,7 @@
     flat = target * capacity + position
     payload = jnp.concatenate([coordinates, element_slot.astype(jnp.float32)[None, :]], axis=0)
     send = jnp.zeros((4, devices * capacity), jnp.float32).at[:, flat].set(payload)
-    arrived = lax.all_to_all(
-        send.reshape(4, devices, capacity),
-        ("gx", "gy", "gz"),
-        split_axis=1,
-        concat_axis=1,
-        tiled=True,
-    )
+    arrived = trade_parts(send.reshape(4, devices, capacity), ("gx", "gy", "gz"), 1, 1)
     width = arrived.shape[2]
     values = interpolate(arrived.reshape(4, -1), fields)
     values = values.reshape(4, devices, width)

time: 267 us -> 322 us (1.21)
  local copies, waits for them, and re-layouts: 138 us -> 192 us
    unnamed x10 -> x73, local copies, waits for them, and re-layouts: 0.59 us -> 51.8 us
    split x0 -> x2, local copies, waits for them, and re-layouts: none -> 8.58 us  [trade_parts(): pieces = jnp.split(x, lax.axis_size(name), axis=split)]
    reshape x1, local copies, waits for them, and re-layouts: 6.68 us -> 0.02 us  [trade_parts(): return jnp.concatenate(received, axis=join)]
where the time goes in v1:
time: 322 us; the launch traced here: 320 us
  local copies, waits for them, and re-layouts  192 us (60%)
  matrix products  72.3 us (22%)
  waiting for transfers between devices  23.8 us (7%)
  other arithmetic  20.2 us (6%)
  starting transfers between devices  10.1 us (3%)
    dot_general x10, matrix products, one_block(): jnp.dot(picker, fields, preferred_element_type=jnp.float32)  71.5 us
    gather x2, local copies, waits for them, and re-layouts, local(): return returned.reshape(4, devices * capacity)[:, flat]  64.7 us
    unnamed x73, local copies, waits for them, and re-layouts  51.8 us
    scatter x1, local copies, waits for them, and re-layouts, local(): jnp.zeros((4, devices * capacity), jnp.float32).at[:, flat].set(payload)  45.3 us
    all_to_all x1, waiting for transfers between devices, local(): lax.all_to_all(values, ('gx', 'gy', 'gz'), split_axis=1, concat_axis=1, t...  12 us
    all_to_all x1, waiting for transfers between devices, trade_parts(): received = lax.all_to_all(jnp.stack(pieces), name, 0, 0)  11.8 us
    split x2, local copies, waits for them, and re-layouts, trade_parts(): pieces = jnp.split(x, lax.axis_size(name), axis=split)  8.58 us
    all_to_all x1, starting transfers between devices, trade_parts(): received = lax.all_to_all(jnp.stack(pieces), name, 0, 0)  7.51 us
  transfers between devices with their start and end apart: 2, of which 2 were waited for; matrix products, arithmetic and copies ran while one was open for 0% of the time, Pallas kernels for 0%

profile of v1, /device:TPU:0, one launch (start us, length us, event | category | flops | bytes accessed | tf_op | source)
XLA Modules:
  0.0 319.7 jit_solution(3954633688500111641)
XLA Ops:
  5.1 5.1 %copy.94 = f32[16384,4]{1,0:T(8,128)} copy(f32[16384,4]{0,1:T(4,128)S(1)} %maximum_bitcast_fusion) | data formatting | bytes 524288 | tf_op jit(solution)/shard_map/concatenate | solution.py:85
  10.2 45.3 %scatter_custom_fusion = f32[4,20480]{0,1:T(8,128)} fusion(s32[16384]{0:T(1024)S(1)} %bitcast.160, f32[16384,4]{1,0:T(8,128)} %copy.94, f32[]{:T(128)} %constant.13.clone.1), kind=kCustom, calls=%fused_computation.42 | custom fusion | bytes 328192 | tf_op jit(solution)/shard_map/scatter | solution.py:86
  55.6 4.2 %fusion.13 = (f32[4,1,640]{0,2,1:T(8,128)}, f32[4,1,640]{0,2,1:T(8,128)}, f32[4,1,640]{0,2,1:T(8,128)}, f32[4,1,640]{0,2,1:T(8,128)}, f32[4,1,640]{0,2,1:T(8,128...) fusion(f32[4,32,640]{0,2,1:T(8,128)} %bitcast.149), kind=kLoop, calls=%fused_computation.90 | loop fusion | bytes 266240 | tf_op jit(solution)/shard_map/split | solution.py:26
  59.8 4.4 %fusion.12 = (f32[4,1,640]{0,2,1:T(8,128)S(1)}, f32[4,1,640]{0,2,1:T(8,128)S(1)}, f32[4,1,640]{0,2,1:T(8,128)S(1)}, f32[4,1,640]{0,2,1:T(8,128)S(1)}, f32[4,1,64...) fusion(f32[4,32,640]{0,2,1:T(8,128)} %bitcast.150), kind=kLoop, calls=%fused_computation.89 | loop fusion | bytes 389120 | tf_op jit(solution)/shard_map/split | solution.py:26
  65.9 1.7 copy.156
  67.6 1.7 copy.157
  116.0 7.5 %all-to-all-start = ((f32[32,4,1,640]{3,1,2,0:T(4,128)}), f32[32,4,1,640]{3,1,2,0:T(4,128)S(1)}, u32[]{:S(2)}, u32[]{:S(2)}) async-start(f32[32,4,1,640]{3,1,2,0:T(4,128)} %constant_dynamic-update-slice_fusion), calls=%async_computation | async-start | bytes 655360 | tf_op jit(solution)/shard_map/all_to_all | solution.py:27
  123.6 11.8 %all-to-all-done = f32[32,4,1,640]{3,1,2,0:T(4,128)S(1)} async-done(((f32[32,4,1,640]{3,1,2,0:T(4,128)}), f32[32,4,1,640]{3,1,2,0:T(4,128)S(1)}, u32[]{:S(2)}, u32[]{:S(2)}) %all-to-all-start) | async-done | bytes 327712 | tf_op jit(solution)/shard_map/all_to_all | solution.py:27
  135.5 99.4 %while.13 = (s32[]{:T(128)}, f32[10,4,2048]{2,1,0:T(4,128)}, f32[10,4,2048]{2,0,1:T(8,128)S(1)}, bf16[128,2048]{1,0:T(8,128)(2,1)}, s32[]{:T(128)}, /*index=5*/f32[8]{0:T(128)S(1)}, s32[]{:T(128)}, s32[]{}, s32[]{}, s32[]{}) while((s32[]{:T(128)}, f32[10,4,2048]{2,1,0:T(4,128)}, ...), condition=%wide.region_4.5_spmd.clone.clone.clone, body=%wide.region_3.4_spmd.sunk.clone.clone.clone.sunk | while | flops 1091790848 | bytes 7209657 | solution.py:64
  136.1 7.2 %multiply_reduce_fusion.7 = f32[2048,256]{0,1:T(8,128)S(1)} fusion(f32[2048,8]{0,1:T(8,128)S(1)} %bitcast_convert_fusion.2, bf16[128,2048]{1,0:T(8,128)(2,1)} %get-tuple-element.288, s32[2048]{0:T(1024)S(1)} %bitcast.164), kind=kOutput, calls=%fused_computation.3.clone.1 | convolution fusion | flops 1090256896 | bytes 2695168 | tf_op jit(solution)/shard_map/while/body/eval_jaxpr/dot_general | solution.py:56
  146.0 7.2 %multiply_reduce_fusion.7 = f32[2048,256]{0,1:T(8,128)S(1)} fusion(f32[2048,8]{0,1:T(8,128)S(1)} %bitcast_convert_fusion.2, bf16[128,2048]{1,0:T(8,128)(2,1)} %get-tuple-element.288, s32[2048]{0:T(1024)S(1)} %bitcast.164), kind=kOutput, calls=%fused_computation.3.clone.1 | convolution fusion | flops 1090256896 | bytes 2695168 | tf_op jit(solution)/shard_map/while/body/eval_jaxpr/dot_general | solution.py:56
  156.0 7.2 %multiply_reduce_fusion.7 = f32[2048,256]{0,1:T(8,128)S(1)} fusion(f32[2048,8]{0,1:T(8,128)S(1)} %bitcast_convert_fusion.2, bf16[128,2048]{1,0:T(8,128)(2,1)} %get-tuple-element.288, s32[2048]{0:T(1024)S(1)} %bitcast.164), kind=kOutput, calls=%fused_computation.3.clone.1 | convolution fusion | flops 1090256896 | bytes 2695168 | tf_op jit(solution)/shard_map/while/body/eval_jaxpr/dot_general | solution.py:56
  165.9 7.2 %multiply_reduce_fusion.7 = f32[2048,256]{0,1:T(8,128)S(1)} fusion(f32[2048,8]{0,1:T(8,128)S(1)} %bitcast_convert_fusion.2, bf16[128,2048]{1,0:T(8,128)(2,1)} %get-tuple-element.288, s32[2048]{0:T(1024)S(1)} %bitcast.164), kind=kOutput, calls=%fused_computation.3.clone.1 | convolution fusion | flops 1090256896 | bytes 2695168 | tf_op jit(solution)/shard_map/while/body/eval_jaxpr/dot_general | solution.py:56
  175.8 7.2 %multiply_reduce_fusion.7 = f32[2048,256]{0,1:T(8,128)S(1)} fusion(f32[2048,8]{0,1:T(8,128)S(1)} %bitcast_convert_fusion.2, bf16[128,2048]{1,0:T(8,128)(2,1)} %get-tuple-element.288, s32[2048]{0:T(1024)S(1)} %bitcast.164), kind=kOutput, calls=%fused_computation.3.clone.1 | convolution fusion | flops 1090256896 | bytes 2695168 | tf_op jit(solution)/shard_map/while/body/eval_jaxpr/dot_general | solution.py:56
  185.8 7.2 %multiply_reduce_fusion.7 = f32[2048,256]{0,1:T(8,128)S(1)} fusion(f32[2048,8]{0,1:T(8,128)S(1)} %bitcast_convert_fusion.2, bf16[128,2048]{1,0:T(8,128)(2,1)} %get-tuple-element.288, s32[2048]{0:T(1024)S(1)} %bitcast.164), kind=kOutput, calls=%fused_computation.3.clone.1 | convolution fusion | flops 1090256896 | bytes 2695168 | tf_op jit(solution)/shard_map/while/body/eval_jaxpr/dot_general | solution.py:56
  195.7 7.2 %multiply_reduce_fusion.7 = f32[2048,256]{0,1:T(8,128)S(1)} fusion(f32[2048,8]{0,1:T(8,128)S(1)} %bitcast_convert_fusion.2, bf16[128,2048]{1,0:T(8,128)(2,1)} %get-tuple-element.288, s32[2048]{0:T(1024)S(1)} %bitcast.164), kind=kOutput, calls=%fused_computation.3.clone.1 | convolution fusion | flops 1090256896 | bytes 2695168 | tf_op jit(solution)/shard_map/while/body/eval_jaxpr/dot_general | solution.py:56
  205.7 7.2 %multiply_reduce_fusion.7 = f32[2048,256]{0,1:T(8,128)S(1)} fusion(f32[2048,8]{0,1:T(8,128)S(1)} %bitcast_convert_fusion.2, bf16[128,2048]{1,0:T(8,128)(2,1)} %get-tuple-element.288, s32[2048]{0:T(1024)S(1)} %bitcast.164), kind=kOutput, calls=%fused_computation.3.clone.1 | convolution fusion | flops 1090256896 | bytes 2695168 | tf_op jit(solution)/shard_map/while/body/eval_jaxpr/dot_general | solution.py:56
  215.6 7.2 %multiply_reduce_fusion.7 = f32[2048,256]{0,1:T(8,128)S(1)} fusion(f32[2048,8]{0,1:T(8,128)S(1)} %bitcast_convert_fusion.2, bf16[128,2048]{1,0:T(8,128)(2,1)} %get-tuple-element.288, s32[2048]{0:T(1024)S(1)} %bitcast.164), kind=kOutput, calls=%fused_computation.3.clone.1 | convolution fusion | flops 1090256896 | bytes 2695168 | tf_op jit(solution)/shard_map/while/body/eval_jaxpr/dot_general | solution.py:56
  225.6 7.2 %multiply_reduce_fusion.7 = f32[2048,256]{0,1:T(8,128)S(1)} fusion(f32[2048,8]{0,1:T(8,128)S(1)} %bitcast_convert_fusion.2, bf16[128,2048]{1,0:T(8,128)(2,1)} %get-tuple-element.288, s32[2048]{0:T(1024)S(1)} %bitcast.164), kind=kOutput, calls=%fused_computation.3.clone.1 | convolution fusion | flops 1090256896 | bytes 2695168 | tf_op jit(solution)/shard_map/while/body/eval_jaxpr/dot_general | solution.py:56
  234.9 2.6 all-to-all-start.1
  237.6 12.0 %all-to-all-done.1 = f32[4,32,640]{2,0,1:T(4,128)S(1)} async-done(((f32[4,32,640]{2,0,1:T(4,128)}), f32[4,32,640]{2,0,1:T(4,128)S(1)}, u32[]{:S(2)}, u32[]{:S(2)}) %all-to-all-start.1) | async-done | bytes 327712 | tf_op jit(solution)/shard_map/all_to_all | solution.py:91
  249.6 5.4 %copy.131 = f32[4,32,640]{0,2,1:T(8,128)} copy(f32[4,32,640]{2,0,1:T(4,128)S(1)} %all-to-all-done.1) | data formatting | bytes 655360 | tf_op jit(solution)/shard_map/all_to_all | solution.py:91
  255.0 58.8 %gather_fusion = f32[16384,4]{1,0:T(8,128)} fusion(f32[4,20480]{0,1:T(8,128)} %bitcast.151, s32[16384]{0:T(1024)S(1)} %broadcast_clamp_fusion), kind=kCustom, calls=%fused_computation | custom fusion | bytes 589824 | tf_op jit(solution)/shard_map/gather | solution.py:92
  313.8 5.9 %copy.132 = f32[4,16384]{1,0:T(4,128)} copy(f32[4,16384]{0,1:T(8,128)} %bitcast.152) | data formatting | bytes 524288 | tf_op jit(solution)/shard_map/gather | solution.py:92
  (299 shorter events, 80.3 us)
Async XLA Ops:
  0.0 4.8 %copy-start = (s32[16384,1]{0,1:T(1,128)S(1)}, s32[16384,1]{0,1:T(1,128)}, u32[]{:S(2)}) copy-start(s32[16384,1]{0,1:T(1,128)} %param.11) | copy-start | bytes 196612
  0.0 5.0 %copy-start.2 = (s32[16384]{0:T(1024)S(1)}, s32[16384]{0:T(1024)}, u32[]{:S(2)}) copy-start(s32[16384]{0:T(1024)} %param.12) | copy-start | bytes 196612
  0.0 5.0 %copy-start.1 = (f32[3,16384]{1,0:T(4,128)S(1)}, f32[3,16384]{1,0:T(4,128)}, u32[]{:S(2)}) copy-start(f32[3,16384]{1,0:T(4,128)} %param.10) | copy-start | bytes 589828
  64.1 71.4 %copy-start.3 = (f32[8]{0:T(128)S(1)}, f32[8]{0:T(128)}, u32[]{:S(2)}) copy-start(f32[8]{0:T(128)} %constant.176) | copy-start | bytes 100
  116.0 19.4 %all-to-all-start = ((f32[32,4,1,640]{3,1,2,0:T(4,128)}), f32[32,4,1,640]{3,1,2,0:T(4,128)S(1)}, u32[]{:S(2)}, u32[]{:S(2)}) async-start(f32[32,4,1,640]{3,1,2,0:T(4,128)} %constant_dynamic-update-slice_fusion), calls=%async_computation | async-start | bytes 655360 | tf_op jit(solution)/shard_map/all_to_all | solution.py:27
  234.9 14.6 %all-to-all-start.1 = ((f32[4,32,640]{2,0,1:T(4,128)}), f32[4,32,640]{2,0,1:T(4,128)S(1)}, u32[]{:S(2)}, u32[]{:S(2)}) async-start(f32[4,32,640]{2,0,1:T(4,128)} %bitcast.47), calls=%async_computation.1 | async-start | bytes 655360 | tf_op jit(solution)/shard_map/all_to_all | solution.py:91
